TPU v7x, 32 devices: a whole 2x2x4 slice. The times are simulated.
32 devices in a mesh: gx: 8 (over z, x), gy: 4 (over y, core).
Axes of the slice: x: 2, y: 2, z: 4, core: 2. Of those that a mesh axis runs over, the one named last changes fastest.
Arguments:
- populations: float32 [19, 48, 32, 128], P(None, 'gx', 'gy'), may hold values from 0.03 to 0.06
- cell_mass: float32 [48, 32, 128], P('gx', 'gy'), may hold values from 0.05 to 1
- cell_flags: int32 [48, 32, 128], P('gx', 'gy'), may hold values from 0 to 2
- bubble: int32 [48, 32, 128], P('gx', 'gy'), may hold values from 0 to 95, as said below
- conversion: int32 [48, 32, 128], P('gx', 'gy'), may hold values 0 or 1
- rest_volume: float32 [96], replicated, may hold values from 256 to 2048
Outputs:
- relaxed_populations: float32 [19, 48, 32, 128], P(None, 'gx', 'gy')
- new_mass: float32 [48, 32, 128], P('gx', 'gy')
- gas_density: float32 [96], replicated
Inputs may be any that keep to these rules, and one draw needn't show every extreme that they name: `cell_flags`: 0 gas, 1 interface, 2 liquid. The bubble that a gas or interface cell belongs to; unused for liquid cells. `conversion`: 1 marks an interface cell that becomes liquid in this step; unused for other cells.
All inputs are finite; a program needn't handle non-finite values. No bound on the sum of `conversion` on one device may be relied on, other than what follows from the above.
Results may differ from a plain program's by a relative error of at most 0.0003.
Values sent between devices are 32-bit elements; how exact they have to be, the bound alone decides.
No kernel may reach another device: no remote copies, remote signals or barrier semaphores. Data moves between devices by JAX's collectives and lax.ppermute only.
A program may use at most 64 MiB of HBM per device.

v0:
```python
import jax
import jax.numpy as jnp
import numpy as np
from jax import lax
from jax.sharding import PartitionSpec as P

VELOCITIES = np.array(
    [
        [0, 0, 0],
        [1, 0, 0],
        [-1, 0, 0],
        [0, 1, 0],
        [0, -1, 0],
        [0, 0, 1],
        [0, 0, -1],
        [1, 1, 0],
        [-1, -1, 0],
        [1, -1, 0],
        [-1, 1, 0],
        [1, 0, 1],
        [-1, 0, -1],
        [1, 0, -1],
        [-1, 0, 1],
        [0, 1, 1],
        [0, -1, -1],
        [0, 1, -1],
        [0, -1, 1],
    ]
)
OPPOSITE = np.array([0, 2, 1, 4, 3, 6, 5, 8, 7, 10, 9, 12, 11, 14, 13, 16, 15, 18, 17])
WEIGHTS = np.array([1.0 / 3.0] + [1.0 / 18.0] * 6 + [1.0 / 36.0] * 12)
RELAX = 1.0 / 0.6
AMBIENT = 2.0


def padded_2(cells, sides, width):
    for axis, dim in sides:
        count = lax.axis_size(axis)
        ends = count - 1
        head = lax.slice_in_dim(cells, 0, width, axis=dim)
        tail = lax.slice_in_dim(cells, cells.shape[dim] - width, cells.shape[dim], axis=dim)
        cells = jnp.concatenate(
            [
                lax.ppermute(tail, axis, [(i, (i + 1) % count) for i in range(ends)]),
                cells,
                lax.ppermute(head, axis, [((i + 1) % count, i) for i in range(ends)]),
            ],
            axis=dim,
        )
    return cells


def moments(populations):
    density = jnp.sum(populations, axis=0)
    lattice = jnp.asarray(VELOCITIES.T, jnp.float32)
    flux = jnp.einsum("kq,qxyz->kxyz", lattice, populations, precision=lax.Precision.HIGHEST)
    return (density, flux / density[None])


def unit_equilibrium(velocity):
    lattice = jnp.asarray(VELOCITIES, jnp.float32)
    project = jnp.einsum("qk,kxyz->qxyz", lattice, velocity, precision=lax.Precision.HIGHEST)
    speed = jnp.sum(velocity * velocity, axis=0)
    weights = jnp.asarray(WEIGHTS, jnp.float32)[:, None, None, None]
    return weights * (1.0 + 3.0 * project + 4.5 * project * project - 1.5 * speed[None])


def window(layer, lane, extent_rows, extent_cols):
    offset_rows, offset_cols, offset_depth = (int(value) for value in VELOCITIES[lane])
    begin_rows, begin_cols = (1 - offset_rows, 1 - offset_cols)
    return jnp.roll(
        layer[begin_rows : begin_rows + extent_rows, begin_cols : begin_cols + extent_cols],
        offset_depth,
        axis=2,
    )


def domain(inside_rows, inside_cols, lane, extent_rows, extent_cols):
    begin_rows, begin_cols = (1 - int(VELOCITIES[lane][0]), 1 - int(VELOCITIES[lane][1]))
    return (
        inside_rows[begin_rows : begin_rows + extent_rows][:, None, None]
        & inside_cols[begin_cols : begin_cols + extent_cols][None, :, None]
    )


def pull_cells(padded, inside_rows, inside_cols, populations, fraction):
    extent_rows, extent_cols = (populations.shape[1], populations.shape[2])
    pulled = [populations[0]]
    gas_side = [jnp.zeros(populations.shape[1:], jnp.bool_)]
    mass_flux = jnp.zeros(populations.shape[1:], jnp.float32)
    targets = jnp.zeros(populations.shape[1:], jnp.float32)
    for lane in range(1, 19):
        source = window(padded[lane], lane, extent_rows, extent_cols)
        source_fraction = window(padded[19], lane, extent_rows, extent_cols)
        source_status = window(padded[20], lane, extent_rows, extent_cols)
        in_domain = domain(inside_rows, inside_cols, lane, extent_rows, extent_cols)
        source_flag = jnp.where(source_status > 2.5, source_status - 3.0, source_status)
        bounced = populations[int(OPPOSITE[lane])]
        pulled.append(jnp.where(in_domain, source, bounced))
        gas_side.append(in_domain & (source_flag < 0.5))
        weight = jnp.where(
            in_domain & (source_flag > 1.5),
            1.0,
            jnp.where(in_domain & (source_flag > 0.5), 0.5 * (fraction + source_fraction), 0.0),
        )
        mass_flux = mass_flux + weight * (source - bounced)
        targets = targets + jnp.where(in_domain & (jnp.abs(source_status - 1.0) < 0.5), 1.0, 0.0)
    return (jnp.stack(pulled), jnp.stack(gas_side), mass_flux, targets)


def settle_cells(
    pulled,
    gas_side,
    populations,
    velocity,
    local_gas,
    cell_mass,
    cell_flags,
    conversion,
    mass_flux,
    targets,
):
    unit = unit_equilibrium(velocity)
    paired = unit + unit[OPPOSITE]
    bounced = populations[OPPOSITE]
    wetted = cell_flags > 0
    passed = jnp.where(gas_side, local_gas[None] * paired - bounced, pulled)
    passed = jnp.where(wetted[None], passed, populations)
    moved_density, moved_velocity = moments(passed)
    relaxed = passed - RELAX * (passed - moved_density[None] * unit_equilibrium(moved_velocity))
    relaxed = jnp.where(wetted[None], relaxed, populations)
    filling = (cell_flags == 1) & (conversion == 1)
    updated = jnp.where(
        cell_flags == 1, cell_mass + mass_flux, jnp.where(cell_flags == 2, moved_density, cell_mass)
    )
    portion = jnp.where(filling, (updated - moved_density) / jnp.maximum(targets, 1.0), 0.0)
    updated = jnp.where(filling, moved_density, updated)
    return (relaxed, updated, portion)


def collect_spill(padded_portion, extent_rows, extent_cols):
    gained = jnp.zeros((extent_rows, extent_cols, padded_portion.shape[2]), jnp.float32)
    for lane in range(1, 19):
        gained = gained + window(padded_portion, lane, extent_rows, extent_cols)
    return gained


def tally_volume(contribution, bubble, count):
    labels = jnp.arange(count, dtype=jnp.int32)
    layer_terms = contribution.reshape(contribution.shape[0], -1)
    layer_labels = bubble.reshape(bubble.shape[0], -1)

    def accumulate(running, layer_pair):
        terms, cell_labels = layer_pair
        indicator = (cell_labels[:, None] == labels[None, :]).astype(jnp.float32)
        summed = jnp.dot(
            terms, indicator, precision=lax.Precision.HIGHEST, preferred_element_type=jnp.float32
        )
        return (running + summed, None)

    running, _ = lax.scan(accumulate, jnp.zeros((count,), jnp.float32), (layer_terms, layer_labels))
    return running


def spread_density(gas_density, bubble):
    labels = jnp.arange(gas_density.shape[0], dtype=jnp.int32)
    layer_labels = bubble.reshape(bubble.shape[0], -1)

    def lookup(cell_labels):
        indicator = (cell_labels[:, None] == labels[None, :]).astype(jnp.float32)
        return jnp.dot(
            indicator,
            gas_density,
            precision=lax.Precision.HIGHEST,
            preferred_element_type=jnp.float32,
        )

    return lax.map(lookup, layer_labels).reshape(bubble.shape)


def total_volume(partial_volume):
    return lax.psum(partial_volume, ("gx", "gy"))


def shards(populations, cell_mass, cell_flags, bubble, conversion, rest_volume):
    extent_rows, extent_cols, extent_depth = (
        populations.shape[1],
        populations.shape[2],
        populations.shape[3],
    )
    density, velocity = moments(populations)
    fraction = jnp.clip(cell_mass / density, 0.0, 1.0)
    status = jnp.where((cell_flags == 1) & (conversion == 1), 4, cell_flags).astype(jnp.float32)
    contribution = jnp.where(cell_flags == 0, 1.0, jnp.where(cell_flags == 1, 1.0 - fraction, 0.0))
    partial_volume = tally_volume(contribution, bubble, rest_volume.shape[0])
    volume = total_volume(partial_volume)
    channels = jnp.concatenate([populations, fraction[None], status[None]], axis=0)
    padded = padded_2(channels, (("gx", 1), ("gy", 2)), 1)
    start_rows = lax.axis_index("gx") * extent_rows + jnp.arange(
        -1, extent_rows + 1, dtype=jnp.int32
    )
    start_cols = lax.axis_index("gy") * extent_cols + jnp.arange(
        -1, extent_cols + 1, dtype=jnp.int32
    )
    inside_rows = (start_rows >= 0) & (start_rows < extent_rows * lax.axis_size("gx"))
    inside_cols = (start_cols >= 0) & (start_cols < extent_cols * lax.axis_size("gy"))
    pulled, gas_side, mass_flux, targets = pull_cells(
        padded, inside_rows, inside_cols, populations, fraction
    )
    gas_density = AMBIENT + rest_volume / jnp.maximum(volume, 1.0)
    local_gas = spread_density(gas_density, bubble)
    relaxed, updated, portion = settle_cells(
        pulled,
        gas_side,
        populations,
        velocity,
        local_gas,
        cell_mass,
        cell_flags,
        conversion,
        mass_flux,
        targets,
    )
    padded_portion = padded_2(portion, (("gx", 0), ("gy", 1)), 1)
    gained = collect_spill(padded_portion, extent_rows, extent_cols)
    receiver = (cell_flags == 1) & (conversion == 0)
    new_mass = jnp.where(receiver, updated + gained, updated)
    return (relaxed, new_mass, gas_density)


def solution(mesh):
    placed = (
        P(None, "gx", "gy", None),
        P("gx", "gy", None),
        P("gx", "gy", None),
        P("gx", "gy", None),
        P("gx", "gy", None),
        P(),
    )
    return jax.shard_map(
        shards,
        mesh=mesh,
        in_specs=placed,
        out_specs=(P(None, "gx", "gy", None), P("gx", "gy", None), P()),
        check_vma=False,
    )
```

profile of v0, /device:TPU:9, one launch (start us, length us, event | category | flops | bytes accessed | tf_op | source)
XLA Modules:
  0.0 112.9 jit_solution(17620983186998840845)
XLA Ops:
  0.6 1.1 reduce_sum.36
  1.8 0.8 convert_bitcast_fusion
  2.6 3.1 %collective-permute-start = (f32[21,1,8,128]{3,2,1,0:T(8,128)S(1)}, f32[21,1,8,128]{3,2,1,0:T(8,128)S(1)}, u32[]{:S(2)}, u32[]{:S(2)}) collective-permute-start(f32[21,1,8,128]{3,2,1,0:T(8,128)S(1)} %get-tuple-element.136), channel_id=1, source_target_pairs={{0,4},{4,8},{8,12},{12,16},{16,20},{20,24},{24,28},{1,5},{5,9},{9,... | collective-permute-start | bytes 258056 | tf_op jit(solution)/shard_map/ppermute | solution.py:44
  5.7 3.1 %collective-permute-start.1 = (f32[21,1,8,128]{3,2,1,0:T(8,128)S(1)}, f32[21,1,8,128]{3,2,1,0:T(8,128)S(1)}, u32[]{:S(2)}, u32[]{:S(2)}) collective-permute-start(f32[21,1,8,128]{3,2,1,0:T(8,128)S(1)} %get-tuple-element.137), channel_id=1, source_target_pairs={{4,0},{8,4},{12,8},{16,12},{20,16},{24,20},{28,24},{5,1},{9,5},{13... | collective-permute-start | bytes 258056 | tf_op jit(solution)/shard_map/ppermute | solution.py:46
  9.0 0.6 broadcast_compare_fusion.1
  9.8 0.6 copy-done.68
  10.4 0.6 multiply_reduce_fusion.1
  11.0 0.6 copy-done.66
  11.7 0.8 fusion.15
  12.6 0.7 copy-done.58
  13.3 2.5 %while.23 = (s32[]{:T(128)}, f32[96]{0:T(128)S(1)}, f32[6,1024]{1,0:T(8,128)S(1)}, s32[6,1024]{1,0:T(8,128)S(1)}, s32[]{:T(128)}, /*index=5*/s32[]{:T(128)}) while((s32[]{:T(128)}, f32[96]{0:T(128)S(1)}, f32[6,1024]{1,0:T(8,128)S(1)}, s32[6,1024]{1,0:T(8,128)S(1)}, s32[]{:T(128)}, /*index=5*/s32[]{:T(128)}) %tuple.207), condition=%wide.region_2.3_spmd.clone, body=%wide.region_1.2_spmd.clone.sunk | while | flops 1278147 | bytes 17367 | solution.py:161
  13.3 0.4 fusion.226
  13.8 0.4 fusion.226
  14.2 0.4 fusion.226
  14.6 0.4 fusion.226
  15.0 0.4 fusion.226
  15.4 0.4 fusion.226
  15.8 39.3 %psum.7 = f32[96]{0:T(128)S(1)} all-reduce(f32[96]{0:T(128)S(1)} %get-tuple-element.57), channel_id=1, replica_groups=mesh['gx'=8,'gy'=4] {'gx','gy'}, use_global_device_ids=true, to_apply=%region_3.4 | all-reduce | flops 96 | bytes 768 | tf_op jit(solution)/shard_map/psum | solution.py:182
  55.1 3.5 %while.22 = (s32[]{:T(128)}, f32[6,1024]{1,0:T(8,128)S(1)}, s32[6,1024]{1,0:T(8,128)S(1)}, f32[96]{0:T(128)S(1)}, s32[]{:T(128)}, /*index=5*/s32[]{:T(128)}) while((s32[]{:T(128)}, f32[6,1024]{1,0:T(8,128)S(1)}, s32[6,1024]{1,0:T(8,128)S(1)}, f32[96]{0:T(128)S(1)}, s32[]{:T(128)}, /*index=5*/s32[]{:T(128)}) %tuple.206), condition=%wide.region_5.6_spmd.clone, body=%wide.region_4.5_spmd.clone.sunk | while | flops 1277954 | bytes 25037 | solution.py:178
  55.2 0.4 fusion.224
  55.7 0.4 fusion.224
  56.3 0.4 fusion.224
  56.9 0.4 fusion.224
  57.5 0.4 fusion.224
  58.1 0.4 fusion.224
  58.6 0.5 copy-done.65
  59.1 0.7 broadcast_and_fusion.3
  59.8 0.6 gather_fusion.1
  60.4 0.6 gather_fusion
  61.2 5.3 %collective-permute-start.2 = (f32[21,8,1,128]{3,2,1,0:T(1,128)S(1)}, f32[21,8,1,128]{3,2,1,0:T(1,128)S(1)}, u32[]{:S(2)}, u32[]{:S(2)}) collective-permute-start(f32[21,8,1,128]{3,2,1,0:T(1,128)S(1)} %get-tuple-element.132), channel_id=1, source_target_pairs={{0,1},{1,2},{2,3},{4,5},{5,6},{6,7},{8,9},{9,10},{10,11},{12,13},{... | collective-permute-start | bytes 258056 | tf_op jit(solution)/shard_map/ppermute | solution.py:44
  66.4 1.9 %collective-permute-start.3 = (f32[21,8,1,128]{3,2,1,0:T(1,128)S(1)}, f32[21,8,1,128]{3,2,1,0:T(1,128)S(1)}, u32[]{:S(2)}, u32[]{:S(2)}) collective-permute-start(f32[21,8,1,128]{3,2,1,0:T(1,128)S(1)} %get-tuple-element.133), channel_id=1, source_target_pairs={{1,0},{2,1},{3,2},{5,4},{6,5},{7,6},{9,8},{10,9},{11,10},{13,12},{... | collective-permute-start | bytes 258056 | tf_op jit(solution)/shard_map/ppermute | solution.py:46
  68.4 3.9 %collective-permute-done.3 = f32[21,8,1,128]{3,2,1,0:T(1,128)S(1)} collective-permute-done((f32[21,8,1,128]{3,2,1,0:T(1,128)S(1)}, f32[21,8,1,128]{3,2,1,0:T(1,128)S(1)}, u32[]{:S(2)}, u32[]{:S(2)}) %collective-permute-start.3) | collective-permute-done | bytes 86048 | tf_op jit(solution)/shard_map/ppermute | solution.py:46
  72.3 0.8 fusion.207
  73.0 0.8 fusion.208
  73.8 0.8 fusion.185
  74.6 0.7 fusion.186
  76.4 0.7 copy-done.53
  77.1 0.7 copy-done.55
  78.0 0.7 copy-done.56
  78.8 0.7 copy-done.62
  79.6 0.7 copy-done.60
  80.3 0.6 copy-done.61
  81.0 0.6 copy-done.59
  81.8 0.7 fusion.180
  82.6 0.7 bitcast_select_fusion.6
  84.1 0.6 copy-done.13
  84.9 0.5 copy-done.7
  85.5 0.7 bitcast_select_fusion
  86.2 0.8 maximum_select_fusion.4
  87.0 0.7 maximum_select_fusion.8
  87.7 3.1 %stack.91 = f32[19,6,8,128]{3,0,2,1:T(8,128)S(1)} concatenate(f32[1,6,8,128]{3,0,2,1:T(1,128)} %bitcast.312, f32[1,6,8,128]{3,0,2,1:T(1,128)} %bitcast.316, f32[1,6,8,128]{3,0,2,1:T(1,128)} %bitcast.315, f32[1,6,8,128]{3,0,2,1:T(1,128)} %bitcast.322, f32[1,6,8,128]{3,0,2,1:T(1,128)} %bitcast.321, f32[1,6,8,128]{3,0,2,1:T(1,128)} %bitcast.325, f32[1,6,8,128]{3,0,2,1:T(1,128)} %bitcast.326, ...), dimensions={0} | concatenate | bytes 933888 | tf_op jit(solution)/shard_map/stack | solution.py:108
  91.2 1.5 %fusion.178 = (f32[6,8,128]{2,1,0:T(8,128)S(1)}, f32[19,6,8,128]{3,0,2,1:T(8,128)S(1)}) fusion(f32[19,6,8,128]{3,2,1,0:T(8,128)S(1)} %copy-done, f32[19,6,8,128]{3,0,2,1:T(8,128)S(1)} %stack.91, f32[19,6,8,128]{3,2,1,0:T(8,128)S(1)} %gather_fusion.1, f32[19,6,8,128]{3,0,2,1:T(8,128)S(1)} %fusion.15, f32[19,6,8,128]{3,2,1,0:T(8,128)S(1)} %gather_fusion, ...), kind=kLoop, calls=%fused_computation.443 | loop fusion | flops 694272 | bytes 2973696 | tf_op jit(solution)/shard_map/reduce_sum | solution.py:54
  93.0 0.3 copy-done.15
  93.4 1.7 %divide_select_fusion = (f32[6,8,128]{2,1,0:T(8,128)S(1)}, f32[6,8,128]{2,1,0:T(8,128)S(1)}) fusion(f32[6,8,128]{2,1,0:T(8,128)S(1)} %get-tuple-element.110, f32[8,10,128]{2,1,0:T(8,128)S(1)} %get-tuple-element.114, pred[6,8]{1,0:T(8,128)(4,1)} %get-tuple-element.290, pred[6,8]{1,0:T(8,128)(4,1)} %get-tuple-element.284, ...), kind=kLoop, calls=%fused_computation.340 | loop fusion | flops 2463744 | bytes 1941936 | tf_op jit(solution)/shard_map/jit(_where)/select_n | solution.py:136
  95.1 3.1 %collective-permute-start.4 = (f32[1,8,128]{2,1,0:T(8,128)S(1)}, f32[1,8,128]{2,1,0:T(8,128)S(1)}, u32[]{:S(2)}, u32[]{:S(2)}) collective-permute-start(f32[1,8,128]{2,1,0:T(8,128)S(1)} %get-tuple-element.282), channel_id=1, source_target_pairs={{0,4},{4,8},{8,12},{12,16},{16,20},{20,24},{24,28},{1,5},{5,9},{9,... | collective-permute-start | bytes 12296 | tf_op jit(solution)/shard_map/ppermute | solution.py:44
  98.3 3.1 %collective-permute-start.5 = (f32[1,8,128]{2,1,0:T(8,128)S(1)}, f32[1,8,128]{2,1,0:T(8,128)S(1)}, u32[]{:S(2)}, u32[]{:S(2)}) collective-permute-start(f32[1,8,128]{2,1,0:T(8,128)S(1)} %get-tuple-element.283), channel_id=1, source_target_pairs={{4,0},{8,4},{12,8},{16,12},{20,16},{24,20},{28,24},{5,1},{9,5},{13... | collective-permute-start | bytes 12296 | tf_op jit(solution)/shard_map/ppermute | solution.py:46
  101.3 0.5 multiply_reduce_fusion
  101.9 0.6 copy-done.57
  102.6 1.0 fusion.23
  103.6 0.9 copy.112
  104.4 2.4 %collective-permute-start.6 = (f32[8,1,128]{2,1,0:T(1,128)S(1)}, f32[8,1,128]{2,1,0:T(1,128)S(1)}, u32[]{:S(2)}, u32[]{:S(2)}) collective-permute-start(f32[8,1,128]{2,1,0:T(1,128)S(1)} %get-tuple-element.271), channel_id=1, source_target_pairs={{0,1},{1,2},{2,3},{4,5},{5,6},{6,7},{8,9},{9,10},{10,11},{12,13},{... | collective-permute-start | bytes 12296 | tf_op jit(solution)/shard_map/ppermute | solution.py:44
  106.9 1.9 %collective-permute-start.7 = (f32[8,1,128]{2,1,0:T(1,128)S(1)}, f32[8,1,128]{2,1,0:T(1,128)S(1)}, u32[]{:S(2)}, u32[]{:S(2)}) collective-permute-start(f32[8,1,128]{2,1,0:T(1,128)S(1)} %get-tuple-element.270), channel_id=1, source_target_pairs={{1,0},{2,1},{3,2},{5,4},{6,5},{7,6},{9,8},{10,9},{11,10},{13,12},{... | collective-permute-start | bytes 12296 | tf_op jit(solution)/shard_map/ppermute | solution.py:46
  109.0 2.8 %collective-permute-done.7 = f32[8,1,128]{2,1,0:T(1,128)S(1)} collective-permute-done((f32[8,1,128]{2,1,0:T(1,128)S(1)}, f32[8,1,128]{2,1,0:T(1,128)S(1)}, u32[]{:S(2)}, u32[]{:S(2)}) %collective-permute-start.7) | collective-permute-done | bytes 4128 | tf_op jit(solution)/shard_map/ppermute | solution.py:46
  112.1 0.8 add_select_fusion
  (222 shorter events, 5.0 us)
Async XLA Ops:
  0.6 2.0 %copy-start = (f32[19,6,8,128]{3,2,1,0:T(8,128)S(1)}, f32[19,6,8,128]{3,2,1,0:T(8,128)}, u32[]{:S(2)}) copy-start(f32[19,6,8,128]{3,2,1,0:T(8,128)} %param.19) | copy-start | bytes 1400836
  0.6 1.1 %copy-start.1 = (s32[6,8,128]{2,1,0:T(8,128)S(1)}, s32[6,8,128]{2,1,0:T(8,128)}, u32[]{:S(2)}) copy-start(s32[6,8,128]{2,1,0:T(8,128)} %param.21) | copy-start | bytes 73732
  1.8 8.0 %copy-start.3 = (f32[6,8,128]{2,1,0:T(8,128)}, f32[6,8,128]{2,1,0:T(8,128)S(1)}, u32[]{:S(2)}) copy-start(f32[6,8,128]{2,1,0:T(8,128)S(1)} %reduce_sum.36) | copy-start | bytes 73732
  1.8 0.8 copy-start.52
  2.6 58.4 %collective-permute-start = (f32[21,1,8,128]{3,2,1,0:T(8,128)S(1)}, f32[21,1,8,128]{3,2,1,0:T(8,128)S(1)}, u32[]{:S(2)}, u32[]{:S(2)}) collective-permute-start(f32[21,1,8,128]{3,2,1,0:T(8,128)S(1)} %get-tuple-element.136), channel_id=1, source_target_pairs={{0,4},{4,8},{8,12},{12,16},{16,20},{20,24},{24,28},{1,5},{5,9},{9,... | collective-permute-start | bytes 258056 | tf_op jit(solution)/shard_map/ppermute | solution.py:44
  5.7 55.3 %collective-permute-start.1 = (f32[21,1,8,128]{3,2,1,0:T(8,128)S(1)}, f32[21,1,8,128]{3,2,1,0:T(8,128)S(1)}, u32[]{:S(2)}, u32[]{:S(2)}) collective-permute-start(f32[21,1,8,128]{3,2,1,0:T(8,128)S(1)} %get-tuple-element.137), channel_id=1, source_target_pairs={{4,0},{8,4},{12,8},{16,12},{20,16},{24,20},{28,24},{5,1},{9,5},{13... | collective-permute-start | bytes 258056 | tf_op jit(solution)/shard_map/ppermute | solution.py:46
  11.0 0.7 copy-start.66
  12.6 0.7 copy-start.58
  15.8 39.3 %copy-start.64 = (f32[96]{0:T(128)S(1)}, f32[96]{0:T(128)}, u32[]{:S(2)}) copy-start(f32[96]{0:T(128)} %param.24) | copy-start | bytes 1156
  59.1 0.7 copy-start.63
  61.2 7.2 %collective-permute-start.2 = (f32[21,8,1,128]{3,2,1,0:T(1,128)S(1)}, f32[21,8,1,128]{3,2,1,0:T(1,128)S(1)}, u32[]{:S(2)}, u32[]{:S(2)}) collective-permute-start(f32[21,8,1,128]{3,2,1,0:T(1,128)S(1)} %get-tuple-element.132), channel_id=1, source_target_pairs={{0,1},{1,2},{2,3},{4,5},{5,6},{6,7},{8,9},{9,10},{10,11},{12,13},{... | collective-permute-start | bytes 258056 | tf_op jit(solution)/shard_map/ppermute | solution.py:44
  66.4 5.8 %collective-permute-start.3 = (f32[21,8,1,128]{3,2,1,0:T(1,128)S(1)}, f32[21,8,1,128]{3,2,1,0:T(1,128)S(1)}, u32[]{:S(2)}, u32[]{:S(2)}) collective-permute-start(f32[21,8,1,128]{3,2,1,0:T(1,128)S(1)} %get-tuple-element.133), channel_id=1, source_target_pairs={{1,0},{2,1},{3,2},{5,4},{6,5},{7,6},{9,8},{10,9},{11,10},{13,12},{... | collective-permute-start | bytes 258056 | tf_op jit(solution)/shard_map/ppermute | solution.py:46
  82.6 0.7 copy-start.5
  82.6 0.7 copy-start.6
  84.9 1.4 %copy-start.11 = (f32[8,10,128]{2,1,0:T(8,128)}, f32[8,10,128]{2,1,0:T(8,128)S(1)}, u32[]{:S(2)}) copy-start(f32[8,10,128]{2,1,0:T(8,128)S(1)} %get-tuple-element.128) | copy-start | bytes 122884
  84.9 1.3 %copy-start.12 = (f32[8,10,128]{2,1,0:T(8,128)}, f32[8,10,128]{2,1,0:T(8,128)S(1)}, u32[]{:S(2)}) copy-start(f32[8,10,128]{2,1,0:T(8,128)S(1)} %get-tuple-element.129) | copy-start | bytes 122884
  87.7 3.1 %copy-start.14 = (pred[19,6,8,128]{3,2,1,0:T(8,128)(4,1)S(1)}, pred[19,6,8,128]{3,2,1,0:T(8,128)(4,1)}, u32[]{:S(2)}) copy-start(pred[19,6,8,128]{3,2,1,0:T(8,128)(4,1)} %copy-done.13) | copy-start | bytes 350212
  90.8 1.9 %copy-start.16 = (f32[6,8,1]{2,1,0:T(8,128)S(1)}, f32[6,8,1]{2,1,0:T(8,128)}, u32[]{:S(2)}) copy-start(f32[6,8,1]{2,1,0:T(8,128)} %get-tuple-element.239) | copy-start | bytes 580
  90.8 1.9 %copy-start.17 = (f32[6,8,1]{2,1,0:T(8,128)S(1)}, f32[6,8,1]{2,1,0:T(8,128)}, u32[]{:S(2)}) copy-start(f32[6,8,1]{2,1,0:T(8,128)} %get-tuple-element.240) | copy-start | bytes 580
  90.8 1.9 %copy-start.18 = (f32[6,8,1]{2,1,0:T(8,128)S(1)}, f32[6,8,1]{2,1,0:T(8,128)}, u32[]{:S(2)}) copy-start(f32[6,8,1]{2,1,0:T(8,128)} %get-tuple-element.241) | copy-start | bytes 580
  90.8 1.9 %copy-start.19 = (f32[6,8,1]{2,1,0:T(8,128)S(1)}, f32[6,8,1]{2,1,0:T(8,128)}, u32[]{:S(2)}) copy-start(f32[6,8,1]{2,1,0:T(8,128)} %get-tuple-element.242) | copy-start | bytes 580
  90.9 1.9 %copy-start.20 = (f32[6,8,1]{2,1,0:T(8,128)S(1)}, f32[6,8,1]{2,1,0:T(8,128)}, u32[]{:S(2)}) copy-start(f32[6,8,1]{2,1,0:T(8,128)} %get-tuple-element.243) | copy-start | bytes 580
  90.9 1.9 %copy-start.21 = (f32[6,8,1]{2,1,0:T(8,128)S(1)}, f32[6,8,1]{2,1,0:T(8,128)}, u32[]{:S(2)}) copy-start(f32[6,8,1]{2,1,0:T(8,128)} %get-tuple-element.244) | copy-start | bytes 580
  90.9 1.9 %copy-start.22 = (f32[6,8,1]{2,1,0:T(8,128)S(1)}, f32[6,8,1]{2,1,0:T(8,128)}, u32[]{:S(2)}) copy-start(f32[6,8,1]{2,1,0:T(8,128)} %get-tuple-element.245) | copy-start | bytes 580
  90.9 1.9 %copy-start.23 = (f32[6,8,1]{2,1,0:T(8,128)S(1)}, f32[6,8,1]{2,1,0:T(8,128)}, u32[]{:S(2)}) copy-start(f32[6,8,1]{2,1,0:T(8,128)} %get-tuple-element.246) | copy-start | bytes 580
  90.9 1.9 %copy-start.24 = (f32[6,8,127]{2,1,0:T(8,128)S(1)}, f32[6,8,127]{2,1,0:T(8,128)}, u32[]{:S(2)}) copy-start(f32[6,8,127]{2,1,0:T(8,128)} %get-tuple-element.247) | copy-start | bytes 73156
  90.9 1.9 %copy-start.25 = (f32[6,8,127]{2,1,0:T(8,128)S(1)}, f32[6,8,127]{2,1,0:T(8,128)}, u32[]{:S(2)}) copy-start(f32[6,8,127]{2,1,0:T(8,128)} %get-tuple-element.258) | copy-start | bytes 73156
  90.9 1.9 %copy-start.26 = (f32[6,8,127]{2,1,0:T(8,128)S(1)}, f32[6,8,127]{2,1,0:T(8,128)}, u32[]{:S(2)}) copy-start(f32[6,8,127]{2,1,0:T(8,128)} %get-tuple-element.259) | copy-start | bytes 73156
  90.9 1.9 %copy-start.27 = (f32[6,8,127]{2,1,0:T(8,128)S(1)}, f32[6,8,127]{2,1,0:T(8,128)}, u32[]{:S(2)}) copy-start(f32[6,8,127]{2,1,0:T(8,128)} %get-tuple-element.260) | copy-start | bytes 73156
  90.9 1.9 %copy-start.28 = (f32[6,8,127]{2,1,0:T(8,128)S(1)}, f32[6,8,127]{2,1,0:T(8,128)}, u32[]{:S(2)}) copy-start(f32[6,8,127]{2,1,0:T(8,128)} %get-tuple-element.261) | copy-start | bytes 73156
  90.9 1.9 %copy-start.29 = (f32[6,8,127]{2,1,0:T(8,128)S(1)}, f32[6,8,127]{2,1,0:T(8,128)}, u32[]{:S(2)}) copy-start(f32[6,8,127]{2,1,0:T(8,128)} %get-tuple-element.262) | copy-start | bytes 73156
  91.0 1.9 %copy-start.30 = (f32[6,8,127]{2,1,0:T(8,128)S(1)}, f32[6,8,127]{2,1,0:T(8,128)}, u32[]{:S(2)}) copy-start(f32[6,8,127]{2,1,0:T(8,128)} %get-tuple-element.263) | copy-start | bytes 73156
  91.0 1.9 %copy-start.31 = (f32[6,8,127]{2,1,0:T(8,128)S(1)}, f32[6,8,127]{2,1,0:T(8,128)}, u32[]{:S(2)}) copy-start(f32[6,8,127]{2,1,0:T(8,128)} %get-tuple-element.264) | copy-start | bytes 73156
  91.0 1.9 %copy-start.32 = (f32[6,8,127]{2,1,0:T(8,128)S(1)}, f32[6,8,127]{2,1,0:T(8,128)}, u32[]{:S(2)}) copy-start(f32[6,8,127]{2,1,0:T(8,128)} %get-tuple-element.265) | copy-start | bytes 73156
  91.0 1.9 %copy-start.33 = (f32[6,8,1]{2,1,0:T(8,128)S(1)}, f32[6,8,1]{2,1,0:T(8,128)}, u32[]{:S(2)}) copy-start(f32[6,8,1]{2,1,0:T(8,128)} %get-tuple-element.168) | copy-start | bytes 580
  91.0 1.9 %copy-start.34 = (f32[6,8,1]{2,1,0:T(8,128)S(1)}, f32[6,8,1]{2,1,0:T(8,128)}, u32[]{:S(2)}) copy-start(f32[6,8,1]{2,1,0:T(8,128)} %get-tuple-element.169) | copy-start | bytes 580
  91.0 1.9 %copy-start.35 = (f32[6,8,1]{2,1,0:T(8,128)S(1)}, f32[6,8,1]{2,1,0:T(8,128)}, u32[]{:S(2)}) copy-start(f32[6,8,1]{2,1,0:T(8,128)} %get-tuple-element.170) | copy-start | bytes 580
  91.0 1.9 %copy-start.36 = (f32[6,8,1]{2,1,0:T(8,128)S(1)}, f32[6,8,1]{2,1,0:T(8,128)}, u32[]{:S(2)}) copy-start(f32[6,8,1]{2,1,0:T(8,128)} %get-tuple-element.171) | copy-start | bytes 580
  91.0 1.9 %copy-start.37 = (f32[6,8,1]{2,1,0:T(8,128)S(1)}, f32[6,8,1]{2,1,0:T(8,128)}, u32[]{:S(2)}) copy-start(f32[6,8,1]{2,1,0:T(8,128)} %get-tuple-element.172) | copy-start | bytes 580
  91.0 1.9 %copy-start.38 = (f32[6,8,1]{2,1,0:T(8,128)S(1)}, f32[6,8,1]{2,1,0:T(8,128)}, u32[]{:S(2)}) copy-start(f32[6,8,1]{2,1,0:T(8,128)} %get-tuple-element.173) | copy-start | bytes 580
  91.0 1.9 %copy-start.39 = (f32[6,8,1]{2,1,0:T(8,128)S(1)}, f32[6,8,1]{2,1,0:T(8,128)}, u32[]{:S(2)}) copy-start(f32[6,8,1]{2,1,0:T(8,128)} %get-tuple-element.174) | copy-start | bytes 580
  91.1 1.9 %copy-start.40 = (f32[6,8,1]{2,1,0:T(8,128)S(1)}, f32[6,8,1]{2,1,0:T(8,128)}, u32[]{:S(2)}) copy-start(f32[6,8,1]{2,1,0:T(8,128)} %get-tuple-element.175) | copy-start | bytes 580
  91.1 1.9 %copy-start.41 = (f32[6,8,1]{2,1,0:T(8,128)S(1)}, f32[6,8,1]{2,1,0:T(8,128)}, u32[]{:S(2)}) copy-start(f32[6,8,1]{2,1,0:T(8,128)} %get-tuple-element.176) | copy-start | bytes 580
  91.1 1.9 %copy-start.42 = (f32[6,8,1]{2,1,0:T(8,128)S(1)}, f32[6,8,1]{2,1,0:T(8,128)}, u32[]{:S(2)}) copy-start(f32[6,8,1]{2,1,0:T(8,128)} %get-tuple-element.177) | copy-start | bytes 580
  91.1 1.9 %copy-start.43 = (f32[6,8,1]{2,1,0:T(8,128)S(1)}, f32[6,8,1]{2,1,0:T(8,128)}, u32[]{:S(2)}) copy-start(f32[6,8,1]{2,1,0:T(8,128)} %get-tuple-element.320) | copy-start | bytes 580
  91.1 1.9 %copy-start.44 = (f32[6,8,127]{2,1,0:T(8,128)S(1)}, f32[6,8,127]{2,1,0:T(8,128)}, u32[]{:S(2)}) copy-start(f32[6,8,127]{2,1,0:T(8,128)} %get-tuple-element.178) | copy-start | bytes 73156
  91.1 1.9 %copy-start.45 = (f32[6,8,127]{2,1,0:T(8,128)S(1)}, f32[6,8,127]{2,1,0:T(8,128)}, u32[]{:S(2)}) copy-start(f32[6,8,127]{2,1,0:T(8,128)} %get-tuple-element.179) | copy-start | bytes 73156
  91.1 1.9 %copy-start.46 = (f32[6,8,127]{2,1,0:T(8,128)S(1)}, f32[6,8,127]{2,1,0:T(8,128)}, u32[]{:S(2)}) copy-start(f32[6,8,127]{2,1,0:T(8,128)} %get-tuple-element.180) | copy-start | bytes 73156
  91.1 1.9 %copy-start.47 = (f32[6,8,127]{2,1,0:T(8,128)S(1)}, f32[6,8,127]{2,1,0:T(8,128)}, u32[]{:S(2)}) copy-start(f32[6,8,127]{2,1,0:T(8,128)} %get-tuple-element.181) | copy-start | bytes 73156
  91.1 1.9 %copy-start.48 = (f32[6,8,127]{2,1,0:T(8,128)S(1)}, f32[6,8,127]{2,1,0:T(8,128)}, u32[]{:S(2)}) copy-start(f32[6,8,127]{2,1,0:T(8,128)} %get-tuple-element.182) | copy-start | bytes 73156
  91.1 1.9 %copy-start.49 = (f32[6,8,127]{2,1,0:T(8,128)S(1)}, f32[6,8,127]{2,1,0:T(8,128)}, u32[]{:S(2)}) copy-start(f32[6,8,127]{2,1,0:T(8,128)} %get-tuple-element.183) | copy-start | bytes 73156
  91.2 1.9 %copy-start.50 = (f32[6,8,127]{2,1,0:T(8,128)S(1)}, f32[6,8,127]{2,1,0:T(8,128)}, u32[]{:S(2)}) copy-start(f32[6,8,127]{2,1,0:T(8,128)} %get-tuple-element.184) | copy-start | bytes 73156
  91.2 1.9 %copy-start.51 = (f32[6,8,127]{2,1,0:T(8,128)S(1)}, f32[6,8,127]{2,1,0:T(8,128)}, u32[]{:S(2)}) copy-start(f32[6,8,127]{2,1,0:T(8,128)} %get-tuple-element.185) | copy-start | bytes 73156
  92.6 0.7 copy-start.15
  92.6 0.7 copy-start.4
  92.7 0.8 copy-start.2
  92.7 0.7 copy-start.54
  95.1 6.2 %copy-start.69 = (f32[3,19,1,1]{1,0,3,2:T(4,128)S(1)}, f32[3,19,1,1]{1,0,3,2:T(4,128)}, u32[]{:S(2)}) copy-start(f32[3,19,1,1]{1,0,3,2:T(4,128)} %constant.139) | copy-start | bytes 688
  95.1 9.3 %collective-permute-start.4 = (f32[1,8,128]{2,1,0:T(8,128)S(1)}, f32[1,8,128]{2,1,0:T(8,128)S(1)}, u32[]{:S(2)}, u32[]{:S(2)}) collective-permute-start(f32[1,8,128]{2,1,0:T(8,128)S(1)} %get-tuple-element.282), channel_id=1, source_target_pairs={{0,4},{4,8},{8,12},{12,16},{16,20},{20,24},{24,28},{1,5},{5,9},{9,... | collective-permute-start | bytes 12296 | tf_op jit(solution)/shard_map/ppermute | solution.py:44
  98.3 6.2 %collective-permute-start.5 = (f32[1,8,128]{2,1,0:T(8,128)S(1)}, f32[1,8,128]{2,1,0:T(8,128)S(1)}, u32[]{:S(2)}, u32[]{:S(2)}) collective-permute-start(f32[1,8,128]{2,1,0:T(8,128)S(1)} %get-tuple-element.283), channel_id=1, source_target_pairs={{4,0},{8,4},{12,8},{16,12},{20,16},{24,20},{28,24},{5,1},{9,5},{13... | collective-permute-start | bytes 12296 | tf_op jit(solution)/shard_map/ppermute | solution.py:46
  101.9 0.7 copy-start.57
  101.9 0.7 copy-start.67
  104.4 4.5 %collective-permute-start.6 = (f32[8,1,128]{2,1,0:T(1,128)S(1)}, f32[8,1,128]{2,1,0:T(1,128)S(1)}, u32[]{:S(2)}, u32[]{:S(2)}) collective-permute-start(f32[8,1,128]{2,1,0:T(1,128)S(1)} %get-tuple-element.271), channel_id=1, source_target_pairs={{0,1},{1,2},{2,3},{4,5},{5,6},{6,7},{8,9},{9,10},{10,11},{12,13},{... | collective-permute-start | bytes 12296 | tf_op jit(solution)/shard_map/ppermute | solution.py:44
  106.9 4.9 %collective-permute-start.7 = (f32[8,1,128]{2,1,0:T(1,128)S(1)}, f32[8,1,128]{2,1,0:T(1,128)S(1)}, u32[]{:S(2)}, u32[]{:S(2)}) collective-permute-start(f32[8,1,128]{2,1,0:T(1,128)S(1)} %get-tuple-element.270), channel_id=1, source_target_pairs={{1,0},{2,1},{3,2},{5,4},{6,5},{7,6},{9,8},{10,9},{11,10},{13,12},{... | collective-permute-start | bytes 12296 | tf_op jit(solution)/shard_map/ppermute | solution.py:46
  (16 other events, 10.3 us)
where the time goes:
time: 114 us; the launch traced here: 113 us
  blocking collectives  39.3 us (34%)
  starting transfers between devices  23.9 us (21%)
  local copies, waits for them, and re-layouts  19.9 us (17%)
  other arithmetic  13 us (11%)
  matrix products  7.83 us (7%)
  waiting for transfers between devices  6.69 us (6%)
  between operations  1.85 us (2%)
    psum x1, blocking collectives, total_volume(): return lax.psum(partial_volume, ('gx', 'gy'))  39.3 us
    ppermute x4, starting transfers between devices, padded_2(): lax.ppermute(tail, axis, [(i, (i + 1) % count) for i in range(ends)])  13.9 us
    unnamed x150, local copies, waits for them, and re-layouts  10.6 us
    ppermute x4, starting transfers between devices, padded_2(): lax.ppermute(head, axis, [((i + 1) % count, i) for i in range(ends)])  9.98 us
    ppermute x4, waiting for transfers between devices, padded_2(): lax.ppermute(head, axis, [((i + 1) % count, i) for i in range(ends)])  6.68 us
    slice x20, local copies, waits for them, and re-layouts, window(): jnp.roll(layer[begin_rows:begin_rows + extent_rows, begin_cols:begin_cols...  4.09 us
    another operation x1, local copies, waits for them, and re-layouts, pull_cells(): return (jnp.stack(pulled), jnp.stack(gas_side), mass_flux, targets)  3.12 us
    select_n x4, other arithmetic, pull_cells(): pulled.append(jnp.where(in_domain, source, bounced))  2.9 us
  transfers between devices with their start and end apart: 8, of which 2 were waited for; matrix products, arithmetic and copies ran while one was open for 11% of the time, Pallas kernels for 0%

commit v1 on v0

--- a/solution.py
+++ b/solution.py
@@ -179,7 +179,7 @@
 
 
 def total_volume(partial_volume):
-    return lax.psum(partial_volume, ("gx", "gy"))
+    return lax.psum(lax.psum(partial_volume, "gx"), "gy")
 
 
 def shards(populations, cell_mass, cell_flags, bubble, conversion, rest_volume):

time: 114 us -> 98 us (0.86)
  blocking collectives: 39.3 us -> 24.2 us
  starting transfers between devices: 23.9 us -> 22.5 us
    psum x1 -> x2, blocking collectives: 39.3 us -> 24.2 us  [total_volume(): return lax.psum(lax.psum(partial_volume, 'gx'), 'gy')]
    ppermute x4, starting transfers between devices: 13.9 us -> 11.3 us  [padded_2(): lax.ppermute(tail, axis, [(i, (i + 1) % count) for i in range(ends)])]
    ppermute x4, starting transfers between devices: 9.98 us -> 11.2 us  [padded_2(): lax.ppermute(head, axis, [((i + 1) % count, i) for i in range(ends)])]
  transfers between devices with their start and end apart: 8 -> 8, of which waited for: 2 -> 2; matrix products, arithmetic and copies ran while one was open for 11% -> 13% of each run, Pallas kernels for 0% -> 0%
where the time goes in v1:
time: 98 us; the launch traced here: 96.4 us
  blocking collectives  24.2 us (25%)
  starting transfers between devices  22.5 us (23%)
  local copies, waits for them, and re-layouts  19.9 us (20%)
  other arithmetic  13.1 us (13%)
  matrix products  7.83 us (8%)
  waiting for transfers between devices  6.69 us (7%)
  between operations  1.85 us (2%)
    psum x2, blocking collectives, total_volume(): return lax.psum(lax.psum(partial_volume, 'gx'), 'gy')  24.2 us
    ppermute x4, starting transfers between devices, padded_2(): lax.ppermute(tail, axis, [(i, (i + 1) % count) for i in range(ends)])  11.3 us
    ppermute x4, starting transfers between devices, padded_2(): lax.ppermute(head, axis, [((i + 1) % count, i) for i in range(ends)])  11.2 us
    unnamed x150, local copies, waits for them, and re-layouts  10.6 us
    ppermute x4, waiting for transfers between devices, padded_2(): lax.ppermute(head, axis, [((i + 1) % count, i) for i in range(ends)])  6.67 us
    slice x20, local copies, waits for them, and re-layouts, window(): jnp.roll(layer[begin_rows:begin_rows + extent_rows, begin_cols:begin_cols...  4.12 us
    another operation x1, local copies, waits for them, and re-layouts, pull_cells(): return (jnp.stack(pulled), jnp.stack(gas_side), mass_flux, targets)  3.12 us
    select_n x4, other arithmetic, pull_cells(): pulled.append(jnp.where(in_domain, source, bounced))  2.94 us
  transfers between devices with their start and end apart: 8, of which 2 were waited for; matrix products, arithmetic and copies ran while one was open for 13% of the time, Pallas kernels for 0%

profile of v1, /device:TPU:9, one launch (start us, length us, event | category | flops | bytes accessed | tf_op | source)
XLA Modules:
  0.0 96.4 jit_solution(17908081078590519700)
XLA Ops:
  0.6 1.1 %reduce_sum.36 = f32[6,8,128]{2,1,0:T(8,128)S(1)} reduce(f32[19,6,8,128]{3,2,1,0:T(8,128)} %param.19, f32[]{:T(128)} %constant.110.clone.1), dimensions={0}, to_apply=%region_0.0 | reduce | flops 110592 | bytes 491524 | tf_op jit(solution)/shard_map/reduce_sum | solution.py:54
  1.8 0.8 convert_bitcast_fusion
  2.6 3.1 %collective-permute-start = (f32[21,1,8,128]{3,2,1,0:T(8,128)S(1)}, f32[21,1,8,128]{3,2,1,0:T(8,128)S(1)}, u32[]{:S(2)}, u32[]{:S(2)}) collective-permute-start(f32[21,1,8,128]{3,2,1,0:T(8,128)S(1)} %get-tuple-element.136), channel_id=1, source_target_pairs={{0,4},{4,8},{8,12},{12,16},{16,20},{20,24},{24,28},{1,5},{5,9},{9,... | collective-permute-start | bytes 258056 | tf_op jit(solution)/shard_map/ppermute | solution.py:44
  5.7 3.1 %collective-permute-start.1 = (f32[21,1,8,128]{3,2,1,0:T(8,128)S(1)}, f32[21,1,8,128]{3,2,1,0:T(8,128)S(1)}, u32[]{:S(2)}, u32[]{:S(2)}) collective-permute-start(f32[21,1,8,128]{3,2,1,0:T(8,128)S(1)} %get-tuple-element.137), channel_id=1, source_target_pairs={{4,0},{8,4},{12,8},{16,12},{20,16},{24,20},{28,24},{5,1},{9,5},{13... | collective-permute-start | bytes 258056 | tf_op jit(solution)/shard_map/ppermute | solution.py:46
  9.0 0.6 broadcast_compare_fusion.1
  9.8 0.6 copy-done.68
  10.4 0.6 multiply_reduce_fusion.1
  11.0 0.6 copy-done.66
  11.7 0.8 fusion.15
  12.6 0.7 copy-done.58
  13.3 2.5 %while.23 = (s32[]{:T(128)}, f32[96]{0:T(128)S(1)}, f32[6,1024]{1,0:T(8,128)S(1)}, s32[6,1024]{1,0:T(8,128)S(1)}, s32[]{:T(128)}, /*index=5*/s32[]{:T(128)}) while((s32[]{:T(128)}, f32[96]{0:T(128)S(1)}, f32[6,1024]{1,0:T(8,128)S(1)}, s32[6,1024]{1,0:T(8,128)S(1)}, s32[]{:T(128)}, /*index=5*/s32[]{:T(128)}) %tuple.207), condition=%wide.region_2.3_spmd.clone, body=%wide.region_1.2_spmd.clone.sunk | while | flops 1278147 | bytes 17367 | solution.py:161
  13.3 0.4 fusion.226
  13.8 0.4 fusion.226
  14.2 0.4 fusion.226
  14.6 0.4 fusion.226
  15.0 0.4 fusion.226
  15.4 0.4 fusion.226
  15.8 14.2 %psum.14 = f32[96]{0:T(128)S(1)} all-reduce(f32[96]{0:T(128)S(1)} %get-tuple-element.57), channel_id=1, replica_groups=mesh['gx'=8,'gy'=4] {'gx'}, use_global_device_ids=true, to_apply=%region_3.4 | all-reduce | flops 96 | bytes 768 | tf_op jit(solution)/shard_map/psum | solution.py:182
  30.0 10.0 %psum.15 = f32[96]{0:T(128)S(1)} all-reduce(f32[96]{0:T(128)S(1)} %psum.14), channel_id=1, replica_groups=mesh['gx'=8,'gy'=4] {'gy'}, use_global_device_ids=true, to_apply=%region_4.5 | all-reduce | flops 96 | bytes 768 | tf_op jit(solution)/shard_map/psum | solution.py:182
  40.0 3.5 %while.22 = (s32[]{:T(128)}, f32[6,1024]{1,0:T(8,128)S(1)}, s32[6,1024]{1,0:T(8,128)S(1)}, f32[96]{0:T(128)S(1)}, s32[]{:T(128)}, /*index=5*/s32[]{:T(128)}) while((s32[]{:T(128)}, f32[6,1024]{1,0:T(8,128)S(1)}, s32[6,1024]{1,0:T(8,128)S(1)}, f32[96]{0:T(128)S(1)}, s32[]{:T(128)}, /*index=5*/s32[]{:T(128)}) %tuple.206), condition=%wide.region_6.7_spmd.clone, body=%wide.region_5.6_spmd.clone.sunk | while | flops 1277954 | bytes 25037 | solution.py:178
  40.1 0.4 fusion.224
  40.6 0.4 fusion.224
  41.2 0.4 fusion.224
  41.8 0.4 fusion.224
  42.4 0.4 fusion.224
  43.0 0.4 fusion.224
  43.5 0.5 copy-done.65
  44.0 0.7 broadcast_and_fusion.3
  44.7 0.6 gather_fusion.1
  45.3 0.6 gather_fusion
  46.1 3.9 %collective-permute-start.2 = (f32[21,8,1,128]{3,2,1,0:T(1,128)S(1)}, f32[21,8,1,128]{3,2,1,0:T(1,128)S(1)}, u32[]{:S(2)}, u32[]{:S(2)}) collective-permute-start(f32[21,8,1,128]{3,2,1,0:T(1,128)S(1)} %get-tuple-element.132), channel_id=1, source_target_pairs={{0,1},{1,2},{2,3},{4,5},{5,6},{6,7},{8,9},{9,10},{10,11},{12,13},{... | collective-permute-start | bytes 258056 | tf_op jit(solution)/shard_map/ppermute | solution.py:44
  50.0 1.9 %collective-permute-start.3 = (f32[21,8,1,128]{3,2,1,0:T(1,128)S(1)}, f32[21,8,1,128]{3,2,1,0:T(1,128)S(1)}, u32[]{:S(2)}, u32[]{:S(2)}) collective-permute-start(f32[21,8,1,128]{3,2,1,0:T(1,128)S(1)} %get-tuple-element.133), channel_id=1, source_target_pairs={{1,0},{2,1},{3,2},{5,4},{6,5},{7,6},{9,8},{10,9},{11,10},{13,12},{... | collective-permute-start | bytes 258056 | tf_op jit(solution)/shard_map/ppermute | solution.py:46
  51.9 3.9 %collective-permute-done.3 = f32[21,8,1,128]{3,2,1,0:T(1,128)S(1)} collective-permute-done((f32[21,8,1,128]{3,2,1,0:T(1,128)S(1)}, f32[21,8,1,128]{3,2,1,0:T(1,128)S(1)}, u32[]{:S(2)}, u32[]{:S(2)}) %collective-permute-start.3) | collective-permute-done | bytes 86048 | tf_op jit(solution)/shard_map/ppermute | solution.py:46
  55.8 0.8 fusion.207
  56.6 0.7 fusion.208
  57.3 0.8 fusion.185
  58.1 0.7 fusion.186
  59.9 0.7 copy-done.53
  60.6 0.7 copy-done.55
  61.5 0.6 copy-done.56
  62.3 0.6 copy-done.62
  63.0 0.7 copy-done.60
  63.8 0.6 copy-done.61
  64.5 0.7 copy-done.59
  65.3 0.7 fusion.180
  66.1 0.7 bitcast_select_fusion.6
  67.6 0.6 copy-done.13
  68.4 0.5 copy-done.7
  69.0 0.8 bitcast_select_fusion
  69.8 0.8 maximum_select_fusion.4
  70.5 0.7 maximum_select_fusion.8
  71.2 3.1 %stack.91 = f32[19,6,8,128]{3,0,2,1:T(8,128)S(1)} concatenate(f32[1,6,8,128]{3,0,2,1:T(1,128)} %bitcast.312, f32[1,6,8,128]{3,0,2,1:T(1,128)} %bitcast.316, f32[1,6,8,128]{3,0,2,1:T(1,128)} %bitcast.315, f32[1,6,8,128]{3,0,2,1:T(1,128)} %bitcast.322, f32[1,6,8,128]{3,0,2,1:T(1,128)} %bitcast.321, f32[1,6,8,128]{3,0,2,1:T(1,128)} %bitcast.325, f32[1,6,8,128]{3,0,2,1:T(1,128)} %bitcast.326, ...), dimensions={0} | concatenate | bytes 933888 | tf_op jit(solution)/shard_map/stack | solution.py:108
  74.7 1.5 %fusion.178 = (f32[6,8,128]{2,1,0:T(8,128)S(1)}, f32[19,6,8,128]{3,0,2,1:T(8,128)S(1)}) fusion(f32[19,6,8,128]{3,2,1,0:T(8,128)S(1)} %copy-done, f32[19,6,8,128]{3,0,2,1:T(8,128)S(1)} %stack.91, f32[19,6,8,128]{3,2,1,0:T(8,128)S(1)} %gather_fusion.1, f32[19,6,8,128]{3,0,2,1:T(8,128)S(1)} %fusion.15, f32[19,6,8,128]{3,2,1,0:T(8,128)S(1)} %gather_fusion, ...), kind=kLoop, calls=%fused_computation.443 | loop fusion | flops 694272 | bytes 2973696 | tf_op jit(solution)/shard_map/reduce_sum | solution.py:54
  77.0 1.7 %divide_select_fusion = (f32[6,8,128]{2,1,0:T(8,128)S(1)}, f32[6,8,128]{2,1,0:T(8,128)S(1)}) fusion(f32[6,8,128]{2,1,0:T(8,128)S(1)} %get-tuple-element.110, f32[8,10,128]{2,1,0:T(8,128)S(1)} %get-tuple-element.114, pred[6,8]{1,0:T(8,128)(4,1)} %get-tuple-element.290, pred[6,8]{1,0:T(8,128)(4,1)} %get-tuple-element.284, ...), kind=kLoop, calls=%fused_computation.340 | loop fusion | flops 2463744 | bytes 1941936 | tf_op jit(solution)/shard_map/jit(_where)/select_n | solution.py:136
  78.7 1.9 %collective-permute-start.4 = (f32[1,8,128]{2,1,0:T(8,128)S(1)}, f32[1,8,128]{2,1,0:T(8,128)S(1)}, u32[]{:S(2)}, u32[]{:S(2)}) collective-permute-start(f32[1,8,128]{2,1,0:T(8,128)S(1)} %get-tuple-element.282), channel_id=1, source_target_pairs={{0,4},{4,8},{8,12},{12,16},{16,20},{20,24},{24,28},{1,5},{5,9},{9,... | collective-permute-start | bytes 12296 | tf_op jit(solution)/shard_map/ppermute | solution.py:44
  80.6 4.3 %collective-permute-start.5 = (f32[1,8,128]{2,1,0:T(8,128)S(1)}, f32[1,8,128]{2,1,0:T(8,128)S(1)}, u32[]{:S(2)}, u32[]{:S(2)}) collective-permute-start(f32[1,8,128]{2,1,0:T(8,128)S(1)} %get-tuple-element.283), channel_id=1, source_target_pairs={{4,0},{8,4},{12,8},{16,12},{20,16},{24,20},{28,24},{5,1},{9,5},{13... | collective-permute-start | bytes 12296 | tf_op jit(solution)/shard_map/ppermute | solution.py:46
  84.9 0.5 multiply_reduce_fusion
  85.5 0.6 copy-done.57
  86.1 1.0 %fusion.23 = f32[19,6,8,128]{3,0,2,1:T(8,128)S(1)} fusion(f32[19,6,8,128]{3,0,2,1:T(8,128)S(1)} %get-tuple-element.111, f32[19,3,1,1]{0,1,3,2:T(4,128)S(1)} %copy-done.67, f32[3,6,8,128]{3,0,2,1:T(4,128)S(1)} %get-tuple-element.302, f32[6,8,128]{2,1,0:T(8,128)S(1)} %broadcast_multiply_fusion, f32[6,8,128]{2,1,0:T(8,128)S(1)} %get-tuple-element.110, ...), kind=kOutput, calls=%fused_computation.33 | convolution fusion | flops 5603328 | bytes 1530160 | tf_op jit(solution)/shard_map/qk,kxyz->qxyz/dot_general | solution.py:62
  87.1 0.9 copy.112
  88.0 2.4 %collective-permute-start.6 = (f32[8,1,128]{2,1,0:T(1,128)S(1)}, f32[8,1,128]{2,1,0:T(1,128)S(1)}, u32[]{:S(2)}, u32[]{:S(2)}) collective-permute-start(f32[8,1,128]{2,1,0:T(1,128)S(1)} %get-tuple-element.271), channel_id=1, source_target_pairs={{0,1},{1,2},{2,3},{4,5},{5,6},{6,7},{8,9},{9,10},{10,11},{12,13},{... | collective-permute-start | bytes 12296 | tf_op jit(solution)/shard_map/ppermute | solution.py:44
  90.4 1.9 %collective-permute-start.7 = (f32[8,1,128]{2,1,0:T(1,128)S(1)}, f32[8,1,128]{2,1,0:T(1,128)S(1)}, u32[]{:S(2)}, u32[]{:S(2)}) collective-permute-start(f32[8,1,128]{2,1,0:T(1,128)S(1)} %get-tuple-element.270), channel_id=1, source_target_pairs={{1,0},{2,1},{3,2},{5,4},{6,5},{7,6},{9,8},{10,9},{11,10},{13,12},{... | collective-permute-start | bytes 12296 | tf_op jit(solution)/shard_map/ppermute | solution.py:46
  92.5 2.8 %collective-permute-done.7 = f32[8,1,128]{2,1,0:T(1,128)S(1)} collective-permute-done((f32[8,1,128]{2,1,0:T(1,128)S(1)}, f32[8,1,128]{2,1,0:T(1,128)S(1)}, u32[]{:S(2)}, u32[]{:S(2)}) %collective-permute-start.7) | collective-permute-done | bytes 4128 | tf_op jit(solution)/shard_map/ppermute | solution.py:46
  95.7 0.8 add_select_fusion
  (223 shorter events, 5.3 us)
Async XLA Ops:
  0.6 2.0 %copy-start = (f32[19,6,8,128]{3,2,1,0:T(8,128)S(1)}, f32[19,6,8,128]{3,2,1,0:T(8,128)}, u32[]{:S(2)}) copy-start(f32[19,6,8,128]{3,2,1,0:T(8,128)} %param.19) | copy-start | bytes 1400836
  0.6 1.1 %copy-start.1 = (s32[6,8,128]{2,1,0:T(8,128)S(1)}, s32[6,8,128]{2,1,0:T(8,128)}, u32[]{:S(2)}) copy-start(s32[6,8,128]{2,1,0:T(8,128)} %param.21) | copy-start | bytes 73732
  1.8 8.0 %copy-start.3 = (f32[6,8,128]{2,1,0:T(8,128)}, f32[6,8,128]{2,1,0:T(8,128)S(1)}, u32[]{:S(2)}) copy-start(f32[6,8,128]{2,1,0:T(8,128)S(1)} %reduce_sum.36) | copy-start | bytes 73732
  1.8 0.8 copy-start.52
  2.6 43.3 %collective-permute-start = (f32[21,1,8,128]{3,2,1,0:T(8,128)S(1)}, f32[21,1,8,128]{3,2,1,0:T(8,128)S(1)}, u32[]{:S(2)}, u32[]{:S(2)}) collective-permute-start(f32[21,1,8,128]{3,2,1,0:T(8,128)S(1)} %get-tuple-element.136), channel_id=1, source_target_pairs={{0,4},{4,8},{8,12},{12,16},{16,20},{20,24},{24,28},{1,5},{5,9},{9,... | collective-permute-start | bytes 258056 | tf_op jit(solution)/shard_map/ppermute | solution.py:44
  5.7 40.2 %collective-permute-start.1 = (f32[21,1,8,128]{3,2,1,0:T(8,128)S(1)}, f32[21,1,8,128]{3,2,1,0:T(8,128)S(1)}, u32[]{:S(2)}, u32[]{:S(2)}) collective-permute-start(f32[21,1,8,128]{3,2,1,0:T(8,128)S(1)} %get-tuple-element.137), channel_id=1, source_target_pairs={{4,0},{8,4},{12,8},{16,12},{20,16},{24,20},{28,24},{5,1},{9,5},{13... | collective-permute-start | bytes 258056 | tf_op jit(solution)/shard_map/ppermute | solution.py:46
  11.0 0.7 copy-start.66
  12.6 0.7 copy-start.58
  30.0 10.0 %copy-start.64 = (f32[96]{0:T(128)S(1)}, f32[96]{0:T(128)}, u32[]{:S(2)}) copy-start(f32[96]{0:T(128)} %param.24) | copy-start | bytes 1156
  44.0 0.7 copy-start.63
  46.1 5.8 %collective-permute-start.2 = (f32[21,8,1,128]{3,2,1,0:T(1,128)S(1)}, f32[21,8,1,128]{3,2,1,0:T(1,128)S(1)}, u32[]{:S(2)}, u32[]{:S(2)}) collective-permute-start(f32[21,8,1,128]{3,2,1,0:T(1,128)S(1)} %get-tuple-element.132), channel_id=1, source_target_pairs={{0,1},{1,2},{2,3},{4,5},{5,6},{6,7},{8,9},{9,10},{10,11},{12,13},{... | collective-permute-start | bytes 258056 | tf_op jit(solution)/shard_map/ppermute | solution.py:44
  50.0 5.8 %collective-permute-start.3 = (f32[21,8,1,128]{3,2,1,0:T(1,128)S(1)}, f32[21,8,1,128]{3,2,1,0:T(1,128)S(1)}, u32[]{:S(2)}, u32[]{:S(2)}) collective-permute-start(f32[21,8,1,128]{3,2,1,0:T(1,128)S(1)} %get-tuple-element.133), channel_id=1, source_target_pairs={{1,0},{2,1},{3,2},{5,4},{6,5},{7,6},{9,8},{10,9},{11,10},{13,12},{... | collective-permute-start | bytes 258056 | tf_op jit(solution)/shard_map/ppermute | solution.py:46
  66.1 0.7 copy-start.5
  66.1 0.7 copy-start.6
  68.4 1.4 %copy-start.11 = (f32[8,10,128]{2,1,0:T(8,128)}, f32[8,10,128]{2,1,0:T(8,128)S(1)}, u32[]{:S(2)}) copy-start(f32[8,10,128]{2,1,0:T(8,128)S(1)} %get-tuple-element.128) | copy-start | bytes 122884
  68.4 1.4 %copy-start.12 = (f32[8,10,128]{2,1,0:T(8,128)}, f32[8,10,128]{2,1,0:T(8,128)S(1)}, u32[]{:S(2)}) copy-start(f32[8,10,128]{2,1,0:T(8,128)S(1)} %get-tuple-element.129) | copy-start | bytes 122884
  71.2 3.1 %copy-start.14 = (pred[19,6,8,128]{3,2,1,0:T(8,128)(4,1)S(1)}, pred[19,6,8,128]{3,2,1,0:T(8,128)(4,1)}, u32[]{:S(2)}) copy-start(pred[19,6,8,128]{3,2,1,0:T(8,128)(4,1)} %copy-done.13) | copy-start | bytes 350212
  74.4 1.9 %copy-start.16 = (f32[6,8,1]{2,1,0:T(8,128)S(1)}, f32[6,8,1]{2,1,0:T(8,128)}, u32[]{:S(2)}) copy-start(f32[6,8,1]{2,1,0:T(8,128)} %get-tuple-element.239) | copy-start | bytes 580
  74.4 1.9 %copy-start.17 = (f32[6,8,1]{2,1,0:T(8,128)S(1)}, f32[6,8,1]{2,1,0:T(8,128)}, u32[]{:S(2)}) copy-start(f32[6,8,1]{2,1,0:T(8,128)} %get-tuple-element.240) | copy-start | bytes 580
  74.4 1.9 %copy-start.18 = (f32[6,8,1]{2,1,0:T(8,128)S(1)}, f32[6,8,1]{2,1,0:T(8,128)}, u32[]{:S(2)}) copy-start(f32[6,8,1]{2,1,0:T(8,128)} %get-tuple-element.241) | copy-start | bytes 580
  74.4 1.9 %copy-start.19 = (f32[6,8,1]{2,1,0:T(8,128)S(1)}, f32[6,8,1]{2,1,0:T(8,128)}, u32[]{:S(2)}) copy-start(f32[6,8,1]{2,1,0:T(8,128)} %get-tuple-element.242) | copy-start | bytes 580
  74.4 1.9 %copy-start.20 = (f32[6,8,1]{2,1,0:T(8,128)S(1)}, f32[6,8,1]{2,1,0:T(8,128)}, u32[]{:S(2)}) copy-start(f32[6,8,1]{2,1,0:T(8,128)} %get-tuple-element.243) | copy-start | bytes 580
  74.4 1.9 %copy-start.21 = (f32[6,8,1]{2,1,0:T(8,128)S(1)}, f32[6,8,1]{2,1,0:T(8,128)}, u32[]{:S(2)}) copy-start(f32[6,8,1]{2,1,0:T(8,128)} %get-tuple-element.244) | copy-start | bytes 580
  74.4 1.9 %copy-start.22 = (f32[6,8,1]{2,1,0:T(8,128)S(1)}, f32[6,8,1]{2,1,0:T(8,128)}, u32[]{:S(2)}) copy-start(f32[6,8,1]{2,1,0:T(8,128)} %get-tuple-element.245) | copy-start | bytes 580
  74.4 1.9 %copy-start.23 = (f32[6,8,1]{2,1,0:T(8,128)S(1)}, f32[6,8,1]{2,1,0:T(8,128)}, u32[]{:S(2)}) copy-start(f32[6,8,1]{2,1,0:T(8,128)} %get-tuple-element.246) | copy-start | bytes 580
  74.4 1.9 %copy-start.24 = (f32[6,8,127]{2,1,0:T(8,128)S(1)}, f32[6,8,127]{2,1,0:T(8,128)}, u32[]{:S(2)}) copy-start(f32[6,8,127]{2,1,0:T(8,128)} %get-tuple-element.247) | copy-start | bytes 73156
  74.5 1.9 %copy-start.25 = (f32[6,8,127]{2,1,0:T(8,128)S(1)}, f32[6,8,127]{2,1,0:T(8,128)}, u32[]{:S(2)}) copy-start(f32[6,8,127]{2,1,0:T(8,128)} %get-tuple-element.258) | copy-start | bytes 73156
  74.5 1.9 %copy-start.26 = (f32[6,8,127]{2,1,0:T(8,128)S(1)}, f32[6,8,127]{2,1,0:T(8,128)}, u32[]{:S(2)}) copy-start(f32[6,8,127]{2,1,0:T(8,128)} %get-tuple-element.259) | copy-start | bytes 73156
  74.5 1.9 %copy-start.27 = (f32[6,8,127]{2,1,0:T(8,128)S(1)}, f32[6,8,127]{2,1,0:T(8,128)}, u32[]{:S(2)}) copy-start(f32[6,8,127]{2,1,0:T(8,128)} %get-tuple-element.260) | copy-start | bytes 73156
  74.5 1.9 %copy-start.28 = (f32[6,8,127]{2,1,0:T(8,128)S(1)}, f32[6,8,127]{2,1,0:T(8,128)}, u32[]{:S(2)}) copy-start(f32[6,8,127]{2,1,0:T(8,128)} %get-tuple-element.261) | copy-start | bytes 73156
  74.5 1.9 %copy-start.29 = (f32[6,8,127]{2,1,0:T(8,128)S(1)}, f32[6,8,127]{2,1,0:T(8,128)}, u32[]{:S(2)}) copy-start(f32[6,8,127]{2,1,0:T(8,128)} %get-tuple-element.262) | copy-start | bytes 73156
  74.5 1.9 %copy-start.30 = (f32[6,8,127]{2,1,0:T(8,128)S(1)}, f32[6,8,127]{2,1,0:T(8,128)}, u32[]{:S(2)}) copy-start(f32[6,8,127]{2,1,0:T(8,128)} %get-tuple-element.263) | copy-start | bytes 73156
  74.5 1.9 %copy-start.31 = (f32[6,8,127]{2,1,0:T(8,128)S(1)}, f32[6,8,127]{2,1,0:T(8,128)}, u32[]{:S(2)}) copy-start(f32[6,8,127]{2,1,0:T(8,128)} %get-tuple-element.264) | copy-start | bytes 73156
  74.5 1.9 %copy-start.32 = (f32[6,8,127]{2,1,0:T(8,128)S(1)}, f32[6,8,127]{2,1,0:T(8,128)}, u32[]{:S(2)}) copy-start(f32[6,8,127]{2,1,0:T(8,128)} %get-tuple-element.265) | copy-start | bytes 73156
  74.5 1.9 %copy-start.33 = (f32[6,8,1]{2,1,0:T(8,128)S(1)}, f32[6,8,1]{2,1,0:T(8,128)}, u32[]{:S(2)}) copy-start(f32[6,8,1]{2,1,0:T(8,128)} %get-tuple-element.168) | copy-start | bytes 580
  74.5 1.9 %copy-start.34 = (f32[6,8,1]{2,1,0:T(8,128)S(1)}, f32[6,8,1]{2,1,0:T(8,128)}, u32[]{:S(2)}) copy-start(f32[6,8,1]{2,1,0:T(8,128)} %get-tuple-element.169) | copy-start | bytes 580
  74.6 1.9 %copy-start.35 = (f32[6,8,1]{2,1,0:T(8,128)S(1)}, f32[6,8,1]{2,1,0:T(8,128)}, u32[]{:S(2)}) copy-start(f32[6,8,1]{2,1,0:T(8,128)} %get-tuple-element.170) | copy-start | bytes 580
  74.6 1.9 %copy-start.36 = (f32[6,8,1]{2,1,0:T(8,128)S(1)}, f32[6,8,1]{2,1,0:T(8,128)}, u32[]{:S(2)}) copy-start(f32[6,8,1]{2,1,0:T(8,128)} %get-tuple-element.171) | copy-start | bytes 580
  74.6 1.9 %copy-start.37 = (f32[6,8,1]{2,1,0:T(8,128)S(1)}, f32[6,8,1]{2,1,0:T(8,128)}, u32[]{:S(2)}) copy-start(f32[6,8,1]{2,1,0:T(8,128)} %get-tuple-element.172) | copy-start | bytes 580
  74.6 1.9 %copy-start.38 = (f32[6,8,1]{2,1,0:T(8,128)S(1)}, f32[6,8,1]{2,1,0:T(8,128)}, u32[]{:S(2)}) copy-start(f32[6,8,1]{2,1,0:T(8,128)} %get-tuple-element.173) | copy-start | bytes 580
  74.6 1.9 %copy-start.39 = (f32[6,8,1]{2,1,0:T(8,128)S(1)}, f32[6,8,1]{2,1,0:T(8,128)}, u32[]{:S(2)}) copy-start(f32[6,8,1]{2,1,0:T(8,128)} %get-tuple-element.174) | copy-start | bytes 580
  74.6 1.9 %copy-start.40 = (f32[6,8,1]{2,1,0:T(8,128)S(1)}, f32[6,8,1]{2,1,0:T(8,128)}, u32[]{:S(2)}) copy-start(f32[6,8,1]{2,1,0:T(8,128)} %get-tuple-element.175) | copy-start | bytes 580
  74.6 1.9 %copy-start.41 = (f32[6,8,1]{2,1,0:T(8,128)S(1)}, f32[6,8,1]{2,1,0:T(8,128)}, u32[]{:S(2)}) copy-start(f32[6,8,1]{2,1,0:T(8,128)} %get-tuple-element.176) | copy-start | bytes 580
  74.6 1.9 %copy-start.42 = (f32[6,8,1]{2,1,0:T(8,128)S(1)}, f32[6,8,1]{2,1,0:T(8,128)}, u32[]{:S(2)}) copy-start(f32[6,8,1]{2,1,0:T(8,128)} %get-tuple-element.177) | copy-start | bytes 580
  74.6 1.9 %copy-start.43 = (f32[6,8,1]{2,1,0:T(8,128)S(1)}, f32[6,8,1]{2,1,0:T(8,128)}, u32[]{:S(2)}) copy-start(f32[6,8,1]{2,1,0:T(8,128)} %get-tuple-element.320) | copy-start | bytes 580
  74.6 1.9 %copy-start.44 = (f32[6,8,127]{2,1,0:T(8,128)S(1)}, f32[6,8,127]{2,1,0:T(8,128)}, u32[]{:S(2)}) copy-start(f32[6,8,127]{2,1,0:T(8,128)} %get-tuple-element.178) | copy-start | bytes 73156
  74.7 1.9 %copy-start.45 = (f32[6,8,127]{2,1,0:T(8,128)S(1)}, f32[6,8,127]{2,1,0:T(8,128)}, u32[]{:S(2)}) copy-start(f32[6,8,127]{2,1,0:T(8,128)} %get-tuple-element.179) | copy-start | bytes 73156
  74.7 1.9 %copy-start.46 = (f32[6,8,127]{2,1,0:T(8,128)S(1)}, f32[6,8,127]{2,1,0:T(8,128)}, u32[]{:S(2)}) copy-start(f32[6,8,127]{2,1,0:T(8,128)} %get-tuple-element.180) | copy-start | bytes 73156
  74.7 1.9 %copy-start.47 = (f32[6,8,127]{2,1,0:T(8,128)S(1)}, f32[6,8,127]{2,1,0:T(8,128)}, u32[]{:S(2)}) copy-start(f32[6,8,127]{2,1,0:T(8,128)} %get-tuple-element.181) | copy-start | bytes 73156
  74.7 1.9 %copy-start.48 = (f32[6,8,127]{2,1,0:T(8,128)S(1)}, f32[6,8,127]{2,1,0:T(8,128)}, u32[]{:S(2)}) copy-start(f32[6,8,127]{2,1,0:T(8,128)} %get-tuple-element.182) | copy-start | bytes 73156
  74.7 1.9 %copy-start.49 = (f32[6,8,127]{2,1,0:T(8,128)S(1)}, f32[6,8,127]{2,1,0:T(8,128)}, u32[]{:S(2)}) copy-start(f32[6,8,127]{2,1,0:T(8,128)} %get-tuple-element.183) | copy-start | bytes 73156
  74.7 1.9 %copy-start.50 = (f32[6,8,127]{2,1,0:T(8,128)S(1)}, f32[6,8,127]{2,1,0:T(8,128)}, u32[]{:S(2)}) copy-start(f32[6,8,127]{2,1,0:T(8,128)} %get-tuple-element.184) | copy-start | bytes 73156
  74.7 1.9 %copy-start.51 = (f32[6,8,127]{2,1,0:T(8,128)S(1)}, f32[6,8,127]{2,1,0:T(8,128)}, u32[]{:S(2)}) copy-start(f32[6,8,127]{2,1,0:T(8,128)} %get-tuple-element.185) | copy-start | bytes 73156
  76.2 0.7 copy-start.15
  76.2 0.7 copy-start.4
  76.2 0.8 copy-start.2
  76.2 0.7 copy-start.54
  78.7 6.2 %copy-start.69 = (f32[3,19,1,1]{1,0,3,2:T(4,128)S(1)}, f32[3,19,1,1]{1,0,3,2:T(4,128)}, u32[]{:S(2)}) copy-start(f32[3,19,1,1]{1,0,3,2:T(4,128)} %constant.139) | copy-start | bytes 688
  78.7 9.3 %collective-permute-start.4 = (f32[1,8,128]{2,1,0:T(8,128)S(1)}, f32[1,8,128]{2,1,0:T(8,128)S(1)}, u32[]{:S(2)}, u32[]{:S(2)}) collective-permute-start(f32[1,8,128]{2,1,0:T(8,128)S(1)} %get-tuple-element.282), channel_id=1, source_target_pairs={{0,4},{4,8},{8,12},{12,16},{16,20},{20,24},{24,28},{1,5},{5,9},{9,... | collective-permute-start | bytes 12296 | tf_op jit(solution)/shard_map/ppermute | solution.py:44
  80.6 7.4 %collective-permute-start.5 = (f32[1,8,128]{2,1,0:T(8,128)S(1)}, f32[1,8,128]{2,1,0:T(8,128)S(1)}, u32[]{:S(2)}, u32[]{:S(2)}) collective-permute-start(f32[1,8,128]{2,1,0:T(8,128)S(1)} %get-tuple-element.283), channel_id=1, source_target_pairs={{4,0},{8,4},{12,8},{16,12},{20,16},{24,20},{28,24},{5,1},{9,5},{13... | collective-permute-start | bytes 12296 | tf_op jit(solution)/shard_map/ppermute | solution.py:46
  85.4 0.7 copy-start.57
  85.4 0.7 copy-start.67
  88.0 4.5 %collective-permute-start.6 = (f32[8,1,128]{2,1,0:T(1,128)S(1)}, f32[8,1,128]{2,1,0:T(1,128)S(1)}, u32[]{:S(2)}, u32[]{:S(2)}) collective-permute-start(f32[8,1,128]{2,1,0:T(1,128)S(1)} %get-tuple-element.271), channel_id=1, source_target_pairs={{0,1},{1,2},{2,3},{4,5},{5,6},{6,7},{8,9},{9,10},{10,11},{12,13},{... | collective-permute-start | bytes 12296 | tf_op jit(solution)/shard_map/ppermute | solution.py:44
  90.4 4.9 %collective-permute-start.7 = (f32[8,1,128]{2,1,0:T(1,128)S(1)}, f32[8,1,128]{2,1,0:T(1,128)S(1)}, u32[]{:S(2)}, u32[]{:S(2)}) collective-permute-start(f32[8,1,128]{2,1,0:T(1,128)S(1)} %get-tuple-element.270), channel_id=1, source_target_pairs={{1,0},{2,1},{3,2},{5,4},{6,5},{7,6},{9,8},{10,9},{11,10},{13,12},{... | collective-permute-start | bytes 12296 | tf_op jit(solution)/shard_map/ppermute | solution.py:46
  (16 other events, 10.3 us)
